TPU v7x, 256 devices: a whole 4x4x8 slice. The times are simulated.
256 devices in a mesh: dp: 16 (over y, x), rows: 16 (over z, core).
Axes of the slice: x: 4, y: 4, z: 8, core: 2. Of those that a mesh axis runs over, the one named last changes fastest.
Arguments:
- grad_out: bfloat16 [8192, 4096], P('dp', 'rows'), may hold values from -0.375 to 0.375
- activations: bfloat16 [8192, 4096], P('dp', 'rows'), may hold values from -6 to 6
- error_feedback: float32 [16, 4096, 4096], P('dp', 'rows'), may hold values from -6 to 6
- momentum: bfloat16 [4096, 4096], P('rows'), may hold values from -1.1953125 to 1.1953125
- right_factor: float32 [4096, 128], P('rows'), may hold values from -0.09375 to 0.09375
Outputs:
- new_error: float32 [16, 4096, 4096], P('dp', 'rows')
- new_momentum: bfloat16 [4096, 4096], P('rows')
- new_right: float32 [4096, 128], P('rows')
All inputs are finite; a program needn't handle non-finite values.
Results may differ from a plain program's by a relative error of at most 0.0012.
Values may be sent and summed in bfloat16 or wider, within the bound.
A program may use at most 64 MiB of HBM per device.

v0:
```python
import jax
import jax.numpy as jnp
from jax import lax
from jax.sharding import PartitionSpec as P

PASSES = 2
MOMENTUM_RATE = 0.9
HIGHEST = lax.Precision.HIGHEST


def from_everyone(value, axis):
    copies = jnp.broadcast_to(value, (lax.axis_size(axis), *value.shape))
    return lax.all_to_all(copies, axis, split_axis=0, concat_axis=0, tiled=True)


def joined_along(tiles, dim):
    lengths = list(tiles.shape[1:])
    lengths[dim] *= tiles.shape[0]
    return jnp.moveaxis(tiles, 0, dim).reshape(lengths)


def gathered_copies(value, axis, dim):
    tiles = from_everyone(value, axis)
    return joined_along(tiles, dim)


def of_everyone(value, axis):
    everything = from_everyone(value, axis)
    return jnp.sum(everything, axis=0)


def total_of_pieces(value, axis):
    return lax.all_gather(value, axis).sum(0)


def cut_along(value, dim, count):
    lengths = value.shape
    tiles = value.reshape(*lengths[:dim], count, lengths[dim] // count, *lengths[dim + 1 :])
    return jnp.moveaxis(tiles, dim, 0)


def sent_and_summed(value, axis, dim):
    count = lax.axis_size(axis)
    tiles = lax.all_to_all(cut_along(value, dim, count), axis, 0, 0, tiled=True)
    return jnp.sum(tiles, axis=0)


def per_device(grad_out, activations, error_feedback, momentum, right_factor):
    replicas = lax.axis_size("dp")
    grad_local = lax.dot_general(
        grad_out,
        lax.all_gather(activations, "rows", axis=1, tiled=True),
        (((0,), (0,)), ((), ())),
        preferred_element_type=jnp.float32,
    )
    merged = grad_local + error_feedback[0]
    right_full = gathered_copies(right_factor, "rows", 0)
    left_factor = None
    own_rows = None
    for pass_index in range(PASSES):
        local_term = jnp.dot(
            merged, right_full, precision=HIGHEST, preferred_element_type=jnp.float32
        )
        left_factor = of_everyone(local_term, "dp") / replicas
        gram_local = jnp.dot(
            left_factor.T, left_factor, precision=HIGHEST, preferred_element_type=jnp.float32
        )
        gram_matrix = total_of_pieces(gram_local, "rows")
        cholesky_lower = jnp.linalg.cholesky(gram_matrix)
        left_factor = jax.scipy.linalg.solve_triangular(cholesky_lower, left_factor.T, lower=True).T
        right_term = lax.dot_general(
            merged,
            left_factor,
            (((0,), (0,)), ((), ())),
            precision=HIGHEST,
            preferred_element_type=jnp.float32,
        )
        own_rows = sent_and_summed(right_term, "rows", 0)
        own_rows = of_everyone(own_rows, "dp") / replicas
        right_full = gathered_copies(own_rows, "rows", 0)
    approx = jnp.dot(
        left_factor, right_full.T, precision=HIGHEST, preferred_element_type=jnp.float32
    )
    new_error = (merged - approx)[None]
    new_momentum = (MOMENTUM_RATE * momentum.astype(jnp.float32) + approx).astype(jnp.bfloat16)
    return (new_error, new_momentum, own_rows)


def solution(mesh):
    return jax.shard_map(
        per_device,
        mesh=mesh,
        in_specs=(
            P("dp", "rows"),
            P("dp", "rows"),
            P("dp", "rows", None),
            P("rows", None),
            P("rows", None),
        ),
        out_specs=(P("dp", "rows", None), P("rows", None), P("rows", None)),
        check_vma=False,
    )
```

profile of v0, /device:TPU:1, one launch (start us, length us, event | category | flops | bytes accessed | tf_op | source)
XLA Modules:
  0.0 616.3 jit_solution(16566047498738973250)
XLA Ops:
  7.9 2.4 broadcast_in_dim.25
  10.3 10.0 %all-to-all-start = ((f32[16,256,128]{2,1,0:T(8,128)}), f32[16,256,128]{2,1,0:T(8,128)S(1)}, u32[]{:S(2)}, u32[]{:S(2)}) async-start(f32[16,256,128]{2,1,0:T(8,128)} %broadcast_in_dim.25), calls=%async_computation | async-start | bytes 4194304 | tf_op jit(solution)/shard_map/all_to_all | solution.py:13
  20.4 75.3 %all-gather.6.cloned.1.call-done = bf16[512,4096]{1,0:T(8,128)(2,1)} async-done(((bf16[512,256]{1,0:T(8,128)(2,1)}), bf16[512,4096]{1,0:T(8,128)(2,1)}) %all-gather.6.cloned.1.call-update) | async-done | bytes 4194320 | tf_op jit(solution)/shard_map/all_gather | solution.py:52
  95.7 6.8 %convolution_add_fusion = f32[256,4096]{1,0:T(8,128)} fusion(bf16[512,256]{1,0:T(8,128)(2,1)S(1)} %copy-done, bf16[512,4096]{1,0:T(8,128)(2,1)} %all-gather.6.cloned.1.call-done, f32[1,256,4096]{2,1,0:T(8,128)} %param.10), kind=kOutput, calls=%fused_computation | convolution fusion | flops 1074790400 | bytes 12845056 | tf_op jit(solution)/shard_map/dot_general | solution.py:50
  102.5 5.9 fusion.26
  108.6 34.5 %all_to_all.45 = f32[16,256,128]{2,1,0:T(8,128)S(1)} all-to-all(f32[16,256,128]{2,1,0:T(8,128)S(1)} %broadcast_in_dim.26), channel_id=1, replica_groups=mesh['dp'=16,'rows'=16] {'dp'}, dimensions={0} | all-to-all | bytes 4194304 | tf_op jit(solution)/shard_map/all_to_all | solution.py:13
  144.4 34.3 %all-gather.8.cloned.1.call-done = f32[2048,128]{1,0:T(8,128)} async-done(((f32[128,128]{1,0:T(8,128)}), f32[2048,128]{1,0:T(8,128)}) %all-gather.8.cloned.1.call-update) | async-done | bytes 1048592 | tf_op jit(solution)/shard_map/all_gather | solution.py:33
  178.7 1.3 reduce_sum.73
  180.1 11.7 %cholesky.44 = f32[128,128]{1,0:T(8,128)S(1)} custom-call(f32[128,128]{1,0:T(8,128)S(1)} %fusion.15), custom_call_target="Cholesky" | custom-call | tf_op jit(solution)/shard_map/jit(cholesky)/cholesky | solution.py:69
  193.2 9.8 %custom-call.6 = f32[1,128,128]{1,2,0:T(8,128)S(1)} custom-call(f32[1,128,128]{2,1,0:T(8,128)S(1)} %fusion.10), custom_call_target="InvertDiagBlocksLowerTriangular" | custom-call | tf_op jit(solution)/shard_map/jit(_solve_triangular)/triangular_solve | solution.py:70
  203.3 8.7 %fusion.27 = f32[4096,128]{1,0:T(8,128)S(1)} fusion(f32[256,4096]{1,0:T(8,128)} %convolution_add_fusion, f32[128,256]{1,0:T(8,128)S(1)} %fusion.2), kind=kOutput, calls=%fused_computation.41 | convolution fusion | flops 1610612736 | bytes 6422528 | tf_op jit(solution)/shard_map/dot_general | solution.py:71
  212.0 55.3 %all_to_all.46 = f32[16,256,128]{2,1,0:T(8,128)S(1)} all-to-all(f32[16,256,128]{2,1,0:T(8,128)S(1)} %bitcast.49), channel_id=1, replica_groups=mesh['dp'=16,'rows'=16] {'rows'}, dimensions={0} | all-to-all | bytes 4194304 | tf_op jit(solution)/shard_map/all_to_all | solution.py:44
  267.6 34.7 %all_to_all.47 = f32[16,256,128]{2,1,0:T(8,128)S(1)} all-to-all(f32[16,256,128]{2,1,0:T(8,128)S(1)} %broadcast_in_dim.27), channel_id=1, replica_groups=mesh['dp'=16,'rows'=16] {'dp'}, dimensions={0} | all-to-all | bytes 4194304 | tf_op jit(solution)/shard_map/all_to_all | solution.py:13
  302.6 54.5 %all_to_all.48 = f32[16,256,128]{2,1,0:T(8,128)S(1)} all-to-all(f32[16,256,128]{2,1,0:T(8,128)S(1)} %broadcast_in_dim.28), channel_id=1, replica_groups=mesh['dp'=16,'rows'=16] {'rows'}, dimensions={0} | all-to-all | bytes 4194304 | tf_op jit(solution)/shard_map/all_to_all | solution.py:13
  357.1 3.5 fusion.28
  360.8 31.1 %all_to_all.49 = f32[16,256,128]{2,1,0:T(8,128)S(1)} all-to-all(f32[16,256,128]{2,1,0:T(8,128)S(1)} %broadcast_in_dim.29), channel_id=1, replica_groups=mesh['dp'=16,'rows'=16] {'dp'}, dimensions={0} | all-to-all | bytes 4194304 | tf_op jit(solution)/shard_map/all_to_all | solution.py:13
  393.0 32.6 %all-gather.10.cloned.1.call-done = f32[2048,128]{1,0:T(8,128)} async-done(((f32[128,128]{1,0:T(8,128)}), f32[2048,128]{1,0:T(8,128)}) %all-gather.10.cloned.1.call-update) | async-done | bytes 1048592 | tf_op jit(solution)/shard_map/all_gather | solution.py:33
  427.0 11.7 %cholesky.55 = f32[128,128]{1,0:T(8,128)S(1)} custom-call(f32[128,128]{1,0:T(8,128)S(1)} %fusion.13), custom_call_target="Cholesky" | custom-call | tf_op jit(solution)/shard_map/jit(cholesky)/cholesky | solution.py:69
  440.1 9.8 %custom-call.7 = f32[1,128,128]{1,2,0:T(8,128)S(1)} custom-call(f32[1,128,128]{2,1,0:T(8,128)S(1)} %fusion.11), custom_call_target="InvertDiagBlocksLowerTriangular" | custom-call | tf_op jit(solution)/shard_map/jit(_solve_triangular)/triangular_solve | solution.py:70
  450.2 8.7 %fusion.29 = f32[4096,128]{1,0:T(8,128)S(1)} fusion(f32[256,4096]{1,0:T(8,128)} %convolution_add_fusion, f32[128,256]{1,0:T(8,128)S(1)} %fusion), kind=kOutput, calls=%fused_computation.43 | convolution fusion | flops 1610612736 | bytes 6422528 | tf_op jit(solution)/shard_map/dot_general | solution.py:71
  458.8 55.3 %all_to_all.50 = f32[16,256,128]{2,1,0:T(8,128)S(1)} all-to-all(f32[16,256,128]{2,1,0:T(8,128)S(1)} %bitcast.51), channel_id=1, replica_groups=mesh['dp'=16,'rows'=16] {'rows'}, dimensions={0} | all-to-all | bytes 4194304 | tf_op jit(solution)/shard_map/all_to_all | solution.py:44
  514.4 34.7 %all_to_all.51 = f32[16,256,128]{2,1,0:T(8,128)S(1)} all-to-all(f32[16,256,128]{2,1,0:T(8,128)S(1)} %broadcast_in_dim.30), channel_id=1, replica_groups=mesh['dp'=16,'rows'=16] {'dp'}, dimensions={0} | all-to-all | bytes 4194304 | tf_op jit(solution)/shard_map/all_to_all | solution.py:13
  549.5 54.5 %all_to_all.52 = f32[16,256,128]{2,1,0:T(8,128)S(1)} all-to-all(f32[16,256,128]{2,1,0:T(8,128)S(1)} %broadcast_in_dim.31), channel_id=1, replica_groups=mesh['dp'=16,'rows'=16] {'rows'}, dimensions={0} | all-to-all | bytes 4194304 | tf_op jit(solution)/shard_map/all_to_all | solution.py:13
  604.0 5.8 add_convert_fusion
  (46 shorter events, 9.7 us)
Async XLA Ops:
  7.2 88.5 %copy-start = (bf16[512,256]{1,0:T(8,128)(2,1)S(1)}, bf16[512,256]{1,0:T(8,128)(2,1)}, u32[]{:S(2)}) copy-start(bf16[512,256]{1,0:T(8,128)(2,1)} %param.8) | copy-start | bytes 786436
  7.2 88.5 %all-gather.6.cloned.1.call-start = ((), (), s32[]{:S(2)}) async-start(), calls=%async_computation.9 | async-start | bytes 4456448 | tf_op jit(solution)/shard_map/all_gather | solution.py:52
  10.3 92.1 %all-to-all-start = ((f32[16,256,128]{2,1,0:T(8,128)}), f32[16,256,128]{2,1,0:T(8,128)S(1)}, u32[]{:S(2)}, u32[]{:S(2)}) async-start(f32[16,256,128]{2,1,0:T(8,128)} %broadcast_in_dim.25), calls=%async_computation | async-start | bytes 4194304 | tf_op jit(solution)/shard_map/all_to_all | solution.py:13
  20.3 158.4 %all-gather.8.cloned.1.call-start = ((), (), s32[]{:S(2)}) async-start(), calls=%async_computation.10 | async-start | bytes 1114112 | tf_op jit(solution)/shard_map/all_gather | solution.py:33
  144.2 281.4 %all-gather.10.cloned.1.call-start = ((), (), s32[]{:S(2)}) async-start(), calls=%async_computation.11 | async-start | bytes 1114112 | tf_op jit(solution)/shard_map/all_gather | solution.py:33
  302.6 54.6 %copy-start.1 = (f32[256,4096]{1,0:T(8,128)S(1)}, f32[256,4096]{1,0:T(8,128)}, u32[]{:S(2)}) copy-start(f32[256,4096]{1,0:T(8,128)} %convolution_add_fusion) | copy-start | bytes 12582916
  549.2 54.8 %copy-start.4 = (f32[256,128]{1,0:T(8,128)}, f32[256,128]{1,0:T(8,128)S(1)}, u32[]{:S(2)}) copy-start(f32[256,128]{1,0:T(8,128)S(1)} %broadcast_multiply_fusion) | copy-start | bytes 393220
  549.2 54.8 %copy-start.3 = (bf16[256,4096]{1,0:T(8,128)(2,1)S(1)}, bf16[256,4096]{1,0:T(8,128)(2,1)}, u32[]{:S(2)}) copy-start(bf16[256,4096]{1,0:T(8,128)(2,1)} %param.11) | copy-start | bytes 6291460
  549.5 54.6 %copy-start.2 = (f32[256,4096]{1,0:T(8,128)S(1)}, f32[256,4096]{1,0:T(8,128)}, u32[]{:S(2)}) copy-start(f32[256,4096]{1,0:T(8,128)} %convolution_add_fusion) | copy-start | bytes 12582916
Sparse Core Ops, SparseCore 0:
  9.7 85.8 all-gather.5
  144.3 34.3 all-gather.7
  393.1 32.4 all-gather.9
where the time goes:
time: 617 us; the launch traced here: 616 us
  blocking collectives  355 us (58%)
  waiting for transfers between devices  143 us (23%)
  other arithmetic  49 us (8%)
  matrix products  41.9 us (7%)
  between operations  14 us (2%)
  starting transfers between devices  10.3 us (2%)
    all_to_all x6, blocking collectives, from_everyone(): return lax.all_to_all(copies, axis, split_axis=0, concat_axis=0, tiled=True)  244 us
    all_to_all x2, blocking collectives, sent_and_summed(): tiles = lax.all_to_all(cut_along(value, dim, count), axis, 0, 0, tiled=True)  111 us
    all_gather x1, waiting for transfers between devices, per_device(): lax.all_gather(activations, 'rows', axis=1, tiled=True)  75.3 us
    all_gather x2, waiting for transfers between devices, total_of_pieces(): return lax.all_gather(value, axis).sum(0)  66.9 us
    another operation x6, other arithmetic, per_device(): cholesky_lower = jnp.linalg.cholesky(gram_matrix)  24.8 us
    another operation x4, other arithmetic, per_device(): jax.scipy.linalg.solve_triangular(cholesky_lower, left_factor.T, lower=True)  20.9 us
    dot_general x2, matrix products, per_device(): lax.dot_general(merged, left_factor, (((0,), (0,)), ((), ())), precision=...  17.3 us
  transfers between devices with their start and end apart: 4, of which 3 were waited for; matrix products, arithmetic and copies ran while one was open for 1% of the time, Pallas kernels for 0%

commit v1 on v0

--- a/solution.py
+++ b/solution.py
@@ -6,6 +6,18 @@
 PASSES = 2
 MOMENTUM_RATE = 0.9
 HIGHEST = lax.Precision.HIGHEST
+
+
+def doubled_up(x, axis, dim):
+    ways, here = (lax.axis_size(axis), lax.axis_index(axis))
+    grown, reach = (x, 1)
+    while reach < ways:
+        theirs = lax.ppermute(grown, axis, [(d, d ^ reach) for d in range(ways)])
+        mine_first = jnp.concatenate([grown, theirs], axis=dim)
+        theirs_first = jnp.concatenate([theirs, grown], axis=dim)
+        grown = jnp.where(here & reach == 0, mine_first, theirs_first)
+        reach = 2 * reach
+    return grown
 
 
 def from_everyone(value, axis):
@@ -49,7 +61,7 @@
     replicas = lax.axis_size("dp")
     grad_local = lax.dot_general(
         grad_out,
-        lax.all_gather(activations, "rows", axis=1, tiled=True),
+        doubled_up(activations, "rows", 1),
         (((0,), (0,)), ((), ())),
         preferred_element_type=jnp.float32,
     )

time: 617 us -> 757 us (1.23); the launches traced: 616 us -> 748 us
  waiting for transfers between devices: 143 us -> 243 us
  local copies, waits for them, and re-layouts: 3.81 us -> 19.8 us
  other arithmetic: 49 us -> 60.1 us
  starting transfers between devices: 10.3 us -> 18.7 us
    ppermute x0 -> x4, waiting for transfers between devices: none -> 142 us  [doubled_up(): theirs = lax.ppermute(grown, axis, [(d, d ^ reach) for d in range(ways)])]
    all_gather x1 -> x0, waiting for transfers between devices: 75.3 us -> none  [per_device(): lax.all_gather(activations, 'rows', axis=1, tiled=True)]
    all_to_all x1, waiting for transfers between devices: 0.01 us -> 22.6 us  [from_everyone(): return lax.all_to_all(copies, axis, split_axis=0, concat_axis=0, tiled=True)]
    all_gather x2, waiting for transfers between devices: 66.9 us -> 78.5 us  [total_of_pieces(): return lax.all_gather(value, axis).sum(0)]
    unnamed x10 -> x14, local copies, waits for them, and re-layouts: 0.03 us -> 11.3 us
    ppermute x0 -> x4, starting transfers between devices: none -> 10.3 us  [doubled_up(): theirs = lax.ppermute(grown, axis, [(d, d ^ reach) for d in range(ways)])]
  transfers between devices with their start and end apart: 4 -> 7, of which waited for: 3 -> 7; matrix products, arithmetic and copies ran while one was open for 1% -> 3% of each run, Pallas kernels for 0% -> 0%
where the time goes in v1:
time: 757 us; the launch traced here: 748 us
  blocking collectives  349 us (46%)
  waiting for transfers between devices  243 us (32%)
  other arithmetic  60.1 us (8%)
  matrix products  43.1 us (6%)
  local copies, waits for them, and re-layouts  19.8 us (3%)
  starting transfers between devices  18.7 us (2%)
  between operations  14.6 us (2%)
    all_to_all x6, blocking collectives, from_everyone(): return lax.all_to_all(copies, axis, split_axis=0, concat_axis=0, tiled=True)  238 us
    ppermute x4, waiting for transfers between devices, doubled_up(): theirs = lax.ppermute(grown, axis, [(d, d ^ reach) for d in range(ways)])  142 us
    all_to_all x2, blocking collectives, sent_and_summed(): tiles = lax.all_to_all(cut_along(value, dim, count), axis, 0, 0, tiled=True)  111 us
    all_gather x2, waiting for transfers between devices, total_of_pieces(): return lax.all_gather(value, axis).sum(0)  78.5 us
    another operation x6, other arithmetic, per_device(): cholesky_lower = jnp.linalg.cholesky(gram_matrix)  24.8 us
    all_to_all x1, waiting for transfers between devices, from_everyone(): return lax.all_to_all(copies, axis, split_axis=0, concat_axis=0, tiled=True)  22.6 us
    another operation x4, other arithmetic, per_device(): jax.scipy.linalg.solve_triangular(cholesky_lower, left_factor.T, lower=True)  20.9 us
    dot_general x2, matrix products, per_device(): jnp.dot(merged, right_full, precision=HIGHEST, preferred_element_type=jnp...  15.3 us
  transfers between devices with their start and end apart: 7, of which 7 were waited for; matrix products, arithmetic and copies ran while one was open for 3% of the time, Pallas kernels for 0%

profile of v1, /device:TPU:1, one launch (start us, length us, event | category | flops | bytes accessed | tf_op | source)
XLA Modules:
  0.0 748.1 jit_solution(10704423115440872313)
XLA Ops:
  13.1 13.1 %collective-permute-done.1 = bf16[512,512]{1,0:T(8,128)(2,1)S(1)} collective-permute-done((bf16[512,512]{1,0:T(8,128)(2,1)S(1)}, bf16[512,512]{1,0:T(8,128)(2,1)S(1)}, u32[]{:S(2)}, u32[]{:S(2)}) %collective-permute-start.1) | collective-permute-done | bytes 524320 | tf_op jit(solution)/shard_map/ppermute | solution.py:15
  29.8 7.8 %all-to-all-start = ((f32[16,256,128]{2,1,0:T(8,128)}), f32[16,256,128]{2,1,0:T(8,128)S(1)}, u32[]{:S(2)}, u32[]{:S(2)}) async-start(f32[16,256,128]{2,1,0:T(8,128)} %broadcast_in_dim.25), calls=%async_computation | async-start | bytes 4194304 | tf_op jit(solution)/shard_map/all_to_all | solution.py:25
  37.7 65.3 %collective-permute-done.2 = bf16[512,1024]{1,0:T(8,128)(2,1)} collective-permute-done((bf16[512,1024]{1,0:T(8,128)(2,1)S(1)}, bf16[512,1024]{1,0:T(8,128)(2,1)}, u32[]{:S(2)}, u32[]{:S(2)}) %collective-permute-start.2) | collective-permute-done | bytes 1048608 | tf_op jit(solution)/shard_map/ppermute | solution.py:15
  117.4 62.1 %collective-permute-done.3 = bf16[512,2048]{1,0:T(8,128)(2,1)} collective-permute-done((bf16[512,2048]{1,0:T(8,128)(2,1)}, bf16[512,2048]{1,0:T(8,128)(2,1)}, u32[]{:S(2)}, u32[]{:S(2)}) %collective-permute-start.3) | collective-permute-done | bytes 2097184 | tf_op jit(solution)/shard_map/ppermute | solution.py:15
  179.6 8.8 %fusion = f32[256,4096]{0,1:T(8,128)} fusion(bf16[512,256]{1,0:T(8,128)(2,1)S(1)} %copy-done, bf16[512,2048]{1,0:T(8,128)(2,1)} %collective-permute-done.3, bf16[512,2048]{1,0:T(8,128)(2,1)} %maximum_select_fusion.2, f32[1,256,4096]{1,2,0:T(8,128)} %copy.18, pred[]{:T(512)S(6)} %eq.12), kind=kOutput, calls=%fused_computation.1 | convolution fusion | flops 1093664768 | bytes 12845057 | tf_op jit(solution)/shard_map/dot_general | solution.py:62
  188.4 22.6 %all-to-all-done = f32[16,256,128]{2,1,0:T(8,128)S(1)} async-done(((f32[16,256,128]{2,1,0:T(8,128)}), f32[16,256,128]{2,1,0:T(8,128)S(1)}, u32[]{:S(2)}, u32[]{:S(2)}) %all-to-all-start) | async-done | bytes 2097184 | tf_op jit(solution)/shard_map/all_to_all | solution.py:25
  211.0 8.5 %fusion.34 = f32[256,128]{1,0:T(8,128)S(1)} fusion(f32[256,4096]{0,1:T(8,128)} %fusion, f32[4096,128]{1,0:T(8,128)S(1)} %bitcast.50), kind=kOutput, calls=%fused_computation.52 | convolution fusion | flops 1610612736 | bytes 6422528 | tf_op jit(solution)/shard_map/dot_general | solution.py:73
  219.7 28.3 %all_to_all.45 = f32[16,256,128]{2,1,0:T(8,128)S(1)} all-to-all(f32[16,256,128]{2,1,0:T(8,128)S(1)} %broadcast_in_dim.26), channel_id=1, replica_groups=mesh['dp'=16,'rows'=16] {'dp'}, dimensions={0} | all-to-all | bytes 4194304 | tf_op jit(solution)/shard_map/all_to_all | solution.py:25
  249.8 45.9 %all-gather.5.cloned.1.call-done = f32[2048,128]{1,0:T(8,128)} async-done(((f32[128,128]{1,0:T(8,128)}), f32[2048,128]{1,0:T(8,128)}) %all-gather.5.cloned.1.call-update) | async-done | bytes 1048592 | tf_op jit(solution)/shard_map/all_gather | solution.py:45
  297.1 11.7 %cholesky.44 = f32[128,128]{1,0:T(8,128)S(1)} custom-call(f32[128,128]{1,0:T(8,128)S(1)} %fusion.22), custom_call_target="Cholesky" | custom-call | tf_op jit(solution)/shard_map/jit(cholesky)/cholesky | solution.py:81
  310.1 9.8 %custom-call.6 = f32[1,128,128]{1,2,0:T(8,128)S(1)} custom-call(f32[1,128,128]{2,1,0:T(8,128)S(1)} %fusion.17), custom_call_target="InvertDiagBlocksLowerTriangular" | custom-call | tf_op jit(solution)/shard_map/jit(_solve_triangular)/triangular_solve | solution.py:82
  325.6 55.3 %all_to_all.46 = f32[16,256,128]{2,1,0:T(8,128)S(1)} all-to-all(f32[16,256,128]{2,1,0:T(8,128)S(1)} %bitcast.51), channel_id=1, replica_groups=mesh['dp'=16,'rows'=16] {'rows'}, dimensions={0} | all-to-all | bytes 4194304 | tf_op jit(solution)/shard_map/all_to_all | solution.py:56
  381.1 34.7 %all_to_all.47 = f32[16,256,128]{2,1,0:T(8,128)S(1)} all-to-all(f32[16,256,128]{2,1,0:T(8,128)S(1)} %broadcast_in_dim.27), channel_id=1, replica_groups=mesh['dp'=16,'rows'=16] {'dp'}, dimensions={0} | all-to-all | bytes 4194304 | tf_op jit(solution)/shard_map/all_to_all | solution.py:25
  416.2 54.7 %all_to_all.48 = f32[16,256,128]{2,1,0:T(8,128)S(1)} all-to-all(f32[16,256,128]{2,1,0:T(8,128)S(1)} %broadcast_in_dim.28), channel_id=1, replica_groups=mesh['dp'=16,'rows'=16] {'rows'}, dimensions={0} | all-to-all | bytes 4194304 | tf_op jit(solution)/shard_map/all_to_all | solution.py:25
  470.9 6.8 fusion.36
  477.9 31.2 %all_to_all.49 = f32[16,256,128]{2,1,0:T(8,128)S(1)} all-to-all(f32[16,256,128]{2,1,0:T(8,128)S(1)} %broadcast_in_dim.29), channel_id=1, replica_groups=mesh['dp'=16,'rows'=16] {'dp'}, dimensions={0} | all-to-all | bytes 4194304 | tf_op jit(solution)/shard_map/all_to_all | solution.py:25
  510.3 32.6 %all-gather.7.cloned.1.call-done = f32[2048,128]{1,0:T(8,128)} async-done(((f32[128,128]{1,0:T(8,128)}), f32[2048,128]{1,0:T(8,128)}) %all-gather.7.cloned.1.call-update) | async-done | bytes 1048592 | tf_op jit(solution)/shard_map/all_gather | solution.py:45
  544.3 11.7 %cholesky.55 = f32[128,128]{1,0:T(8,128)S(1)} custom-call(f32[128,128]{1,0:T(8,128)S(1)} %fusion.20), custom_call_target="Cholesky" | custom-call | tf_op jit(solution)/shard_map/jit(cholesky)/cholesky | solution.py:81
  557.4 9.8 %custom-call.7 = f32[1,128,128]{1,2,0:T(8,128)S(1)} custom-call(f32[1,128,128]{2,1,0:T(8,128)S(1)} %fusion.18), custom_call_target="InvertDiagBlocksLowerTriangular" | custom-call | tf_op jit(solution)/shard_map/jit(_solve_triangular)/triangular_solve | solution.py:82
  572.8 55.3 %all_to_all.50 = f32[16,256,128]{2,1,0:T(8,128)S(1)} all-to-all(f32[16,256,128]{2,1,0:T(8,128)S(1)} %bitcast.53), channel_id=1, replica_groups=mesh['dp'=16,'rows'=16] {'rows'}, dimensions={0} | all-to-all | bytes 4194304 | tf_op jit(solution)/shard_map/all_to_all | solution.py:56
  628.4 34.7 %all_to_all.51 = f32[16,256,128]{2,1,0:T(8,128)S(1)} all-to-all(f32[16,256,128]{2,1,0:T(8,128)S(1)} %broadcast_in_dim.30), channel_id=1, replica_groups=mesh['dp'=16,'rows'=16] {'dp'}, dimensions={0} | all-to-all | bytes 4194304 | tf_op jit(solution)/shard_map/all_to_all | solution.py:25
  663.4 54.6 %all_to_all.52 = f32[16,256,128]{2,1,0:T(8,128)S(1)} all-to-all(f32[16,256,128]{2,1,0:T(8,128)S(1)} %broadcast_in_dim.31), channel_id=1, replica_groups=mesh['dp'=16,'rows'=16] {'rows'}, dimensions={0} | all-to-all | bytes 4194304 | tf_op jit(solution)/shard_map/all_to_all | solution.py:25
  718.1 5.7 add_convert_fusion
  729.4 6.0 subtract_bitcast_fusion
  (60 shorter events, 56.4 us)
Async XLA Ops:
  7.2 172.4 %copy-start = (bf16[512,256]{1,0:T(8,128)(2,1)S(1)}, bf16[512,256]{1,0:T(8,128)(2,1)}, u32[]{:S(2)}) copy-start(bf16[512,256]{1,0:T(8,128)(2,1)} %param.8) | copy-start | bytes 786436
  7.2 21.1 %copy-start.5 = (f32[256,128]{1,0:T(8,128)S(1)}, f32[256,128]{1,0:T(8,128)}, u32[]{:S(2)}) copy-start(f32[256,128]{1,0:T(8,128)} %param.12) | copy-start | bytes 393220
  7.2 4.7 collective-permute-start
  13.0 13.2 %collective-permute-start.1 = (bf16[512,512]{1,0:T(8,128)(2,1)S(1)}, bf16[512,512]{1,0:T(8,128)(2,1)S(1)}, u32[]{:S(2)}, u32[]{:S(2)}) collective-permute-start(bf16[512,512]{1,0:T(8,128)(2,1)S(1)} %maximum_select_fusion.4), channel_id=1, source_target_pairs={{0,2},{1,3},{2,0},{3,1},{4,6},{5,7},{6,4},{7,5},{8,10},{9,11},{10,... | collective-permute-start | bytes 1572872 | tf_op jit(solution)/shard_map/ppermute | solution.py:15
  26.5 76.5 %collective-permute-start.2 = (bf16[512,1024]{1,0:T(8,128)(2,1)S(1)}, bf16[512,1024]{1,0:T(8,128)(2,1)}, u32[]{:S(2)}, u32[]{:S(2)}) collective-permute-start(bf16[512,1024]{1,0:T(8,128)(2,1)S(1)} %maximum_select_fusion.3), channel_id=1, source_target_pairs={{0,4},{1,5},{2,6},{3,7},{4,0},{5,1},{6,2},{7,3},{8,12},{9,13},{10,... | collective-permute-start | bytes 3145736 | tf_op jit(solution)/shard_map/ppermute | solution.py:15
  29.8 181.2 %all-to-all-start = ((f32[16,256,128]{2,1,0:T(8,128)}), f32[16,256,128]{2,1,0:T(8,128)S(1)}, u32[]{:S(2)}, u32[]{:S(2)}) async-start(f32[16,256,128]{2,1,0:T(8,128)} %broadcast_in_dim.25), calls=%async_computation | async-start | bytes 4194304 | tf_op jit(solution)/shard_map/all_to_all | solution.py:25
  37.6 258.0 %all-gather.5.cloned.1.call-start = ((), (), s32[]{:S(2)}) async-start(), calls=%async_computation.9 | async-start | bytes 1114112 | tf_op jit(solution)/shard_map/all_gather | solution.py:45
  106.6 72.9 %collective-permute-start.3 = (bf16[512,2048]{1,0:T(8,128)(2,1)}, bf16[512,2048]{1,0:T(8,128)(2,1)}, u32[]{:S(2)}, u32[]{:S(2)}) collective-permute-start(bf16[512,2048]{1,0:T(8,128)(2,1)} %maximum_select_fusion.2), channel_id=1, source_target_pairs={{0,8},{1,9},{2,10},{3,11},{4,12},{5,13},{6,14},{7,15},{8,0},{9,1},... | collective-permute-start | bytes 6291464 | tf_op jit(solution)/shard_map/ppermute | solution.py:15
  249.2 293.7 %all-gather.7.cloned.1.call-start = ((), (), s32[]{:S(2)}) async-start(), calls=%async_computation.10 | async-start | bytes 1114112 | tf_op jit(solution)/shard_map/all_gather | solution.py:45
  416.1 54.7 %copy-start.2 = (f32[256,4096]{0,1:T(8,128)S(1)}, f32[256,4096]{0,1:T(8,128)}, u32[]{:S(2)}) copy-start(f32[256,4096]{0,1:T(8,128)} %fusion) | copy-start | bytes 12582916
  663.2 54.9 %copy-start.4 = (f32[256,128]{1,0:T(8,128)}, f32[256,128]{1,0:T(8,128)S(1)}, u32[]{:S(2)}) copy-start(f32[256,128]{1,0:T(8,128)S(1)} %broadcast_multiply_fusion) | copy-start | bytes 393220
  663.4 54.7 %copy-start.3 = (bf16[256,4096]{1,0:T(8,128)(2,1)S(1)}, bf16[256,4096]{1,0:T(8,128)(2,1)}, u32[]{:S(2)}) copy-start(bf16[256,4096]{1,0:T(8,128)(2,1)} %param.11) | copy-start | bytes 6291460
  735.3 5.6 copy-start.1
Sparse Core Ops, SparseCore 0:
  249.3 46.2 all-gather.4
  510.4 32.4 all-gather.6
